TPU v7x, 32 devices: a whole 2x2x4 slice. The times are simulated.
32 devices in a mesh: role: 2 (over x), ctx: 4 (over z), head: 4 (over y, core).
Axes of the slice: x: 2, y: 2, z: 4, core: 2. Of those that a mesh axis runs over, the one named last changes fastest.
Arguments:
- tokens: bfloat16 [2, 256, 7168], P('role', 'ctx', 'head'), may hold values from -6 to 6
- latent_cache: bfloat16 [192, 576], P('ctx'), may hold values from -400 to 400
- offset: int32 [1], replicated, may hold values from 49 to 192
- bounds: int32 [256], P('ctx'), may hold values from 1 to 448
- query_down: bfloat16 [7168, 1536], P('head'), may hold values from -0.0625 to 0.0625
- latent_down_weight: bfloat16 [7168, 576], P('head'), may hold values from -0.0625 to 0.0625
- query_gain: float32 [1536], replicated, may hold values from 0.25 to 1.75
- latent_norm_gain: float32 [512], replicated, may hold values from 0.25 to 1.75
- query_up: bfloat16 [1536, 24576], P(None, 'head'), may hold values from -0.15625 to 0.15625
- key_up_transposed: bfloat16 [128, 128, 512], P('head'), may hold values from -0.5 to 0.5
- value_up_weight: bfloat16 [128, 512, 128], P('head'), may hold values from -0.25 to 0.25
Outputs:
- attended: bfloat16 [2, 256, 16384], P('role', 'ctx', 'head')
Inputs may be any that keep to these rules, and one draw needn't show every extreme that they name: `bounds`: A continuation row at position p sees keys at positions below p and itself. Cache slots from offset on are unused; the block's tokens sit at positions offset to offset + 255.
All inputs are finite; a program needn't handle non-finite values.
Results may differ from a plain program's by a relative error of at most 0.02.
Values may be sent and summed in bfloat16 or wider, within the bound.
No kernel may reach another device: no remote copies, remote signals or barrier semaphores. Data moves between devices by JAX's collectives and lax.ppermute only.
A program may use at most 128 MiB of HBM per device.

v0:
```python
import jax
import jax.numpy as jnp
from jax import lax
from jax.sharding import PartitionSpec as P

LATENT_WIDTH = 512
ROTARY_DIM = 64
PLAIN_QUERY_DIM = 128
VALUE_HEAD_SIZE = 128
EPS = 1e-06


def passed_along(value, axis, steps):
    count = lax.axis_size(axis)
    leading, last = (max(0, -steps), min(count, count - steps))
    return lax.ppermute(value, axis, [(source, source + steps) for source in range(leading, last)])


def root_mean_norm(value_rows, gain):
    return (
        value_rows
        * lax.rsqrt(jnp.mean(value_rows * value_rows, axis=-1, keepdims=True) + EPS)
        * gain
    )


def apply_rotary(value_rows, token_positions):
    half = value_rows.shape[-1] // 2
    freqs = 10000.0 ** (-jnp.arange(half, dtype=jnp.float32) / half)
    angles = token_positions.astype(jnp.float32)[:, None] * freqs[None, :]
    if value_rows.ndim == 3:
        angles = angles[:, None, :]
    first = value_rows[..., :half]
    second_half = value_rows[..., half:]
    cosine = jnp.cos(angles)
    sine = jnp.sin(angles)
    return jnp.concatenate(
        [first * cosine - second_half * sine, first * sine + second_half * cosine], axis=-1
    )


def finish_latents(query_lat, key_value_latent, token_positions, query_gain, latent_norm_gain):
    query_norm = root_mean_norm(query_lat, query_gain).astype(jnp.bfloat16)
    latent_vector = root_mean_norm(key_value_latent[:, :LATENT_WIDTH], latent_norm_gain)
    rotary_key_part = apply_rotary(key_value_latent[:, LATENT_WIDTH:], token_positions)
    return (
        query_norm,
        jnp.concatenate([latent_vector, rotary_key_part], axis=-1).astype(jnp.bfloat16),
    )


def local(
    tokens,
    latent_cache,
    offset,
    bounds,
    query_down,
    latent_down_weight,
    query_gain,
    latent_norm_gain,
    query_up,
    key_up_transposed,
    value_up_weight,
):
    count_of_rows = tokens.shape[1]
    cache_rows = latent_cache.shape[0]
    local_head_count = key_up_transposed.shape[0]
    role_index = lax.axis_index("role")
    block_start = offset[0]
    local_rows = lax.axis_index("ctx") * count_of_rows + jnp.arange(count_of_rows, dtype=jnp.int32)
    token_positions = jnp.where(role_index == 0, block_start + local_rows, bounds)
    inputs = tokens[0]
    query_part = jnp.dot(inputs, query_down, preferred_element_type=jnp.float32)
    kv_part = jnp.dot(inputs, latent_down_weight, preferred_element_type=jnp.float32)
    query_lat, key_value_latent = (
        lax.psum_scatter(query_part, "head", scatter_dimension=0, tiled=True),
        lax.psum_scatter(kv_part, "head", scatter_dimension=0, tiled=True),
    )
    share_rows = query_lat.shape[0]
    share_pos = lax.dynamic_slice_in_dim(
        token_positions, lax.axis_index("head") * share_rows, share_rows
    )
    query_share, key_share = finish_latents(
        query_lat, key_value_latent, share_pos, query_gain, latent_norm_gain
    )
    query_norm, self_key_row = (
        lax.all_gather(query_share, "head", axis=0, tiled=True),
        lax.all_gather(key_share, "head", axis=0, tiled=True),
    )
    queries = jnp.dot(query_norm, query_up, preferred_element_type=jnp.float32)
    queries = queries.reshape(count_of_rows, local_head_count, PLAIN_QUERY_DIM + ROTARY_DIM)
    query_nope = queries[..., :PLAIN_QUERY_DIM].astype(jnp.bfloat16)
    query_rot = apply_rotary(queries[..., PLAIN_QUERY_DIM:], token_positions).astype(jnp.bfloat16)
    absorbed = jnp.einsum(
        "rhn,hnc->rhc", query_nope, key_up_transposed, preferred_element_type=jnp.float32
    ).astype(jnp.bfloat16)
    complete_query = jnp.concatenate([absorbed, query_rot], axis=-1)
    softmax_scale = (PLAIN_QUERY_DIM + ROTARY_DIM) ** (-0.5)
    self_score = jnp.sum(
        complete_query.astype(jnp.float32) * self_key_row.astype(jnp.float32)[:, None, :], axis=-1
    )
    self_score = self_score.reshape(count_of_rows * local_head_count) * softmax_scale
    flattened_query = complete_query.reshape(
        count_of_rows * local_head_count, LATENT_WIDTH + ROTARY_DIM
    )
    row_limits = jnp.repeat(token_positions, local_head_count)
    relayed = passed_along(self_key_row, "role", 1)
    block_key = jnp.where(role_index == 0, self_key_row, relayed)
    per_shard = cache_rows + count_of_rows
    local_keys = jnp.concatenate([latent_cache, block_key], axis=0)
    slice_portion = lax.all_gather(local_keys, "ctx", axis=0, tiled=True)
    global_index = jnp.arange(slice_portion.shape[0], dtype=jnp.int32)
    shard_index = global_index // per_shard
    within = global_index % per_shard
    is_cached = within < cache_rows
    key_pos = jnp.where(
        is_cached,
        shard_index * cache_rows + within,
        block_start + shard_index * count_of_rows + within - cache_rows,
    )
    key_valid = jnp.where(is_cached, key_pos < block_start, True)
    running_max = self_score
    running_sum = jnp.ones_like(self_score)
    output_accumulate = jnp.repeat(
        self_key_row[:, :LATENT_WIDTH].astype(jnp.float32), local_head_count, axis=0
    )
    scores = (
        jnp.dot(flattened_query, slice_portion.T, preferred_element_type=jnp.float32)
        * softmax_scale
    )
    key_mask = key_valid[None, :] & (key_pos[None, :] < row_limits[:, None])
    new_max = jnp.maximum(running_max, jnp.max(jnp.where(key_mask, scores, -jnp.inf), axis=-1))
    attention_weights = jnp.where(key_mask, jnp.exp(scores - new_max[:, None]), 0.0)
    fading = jnp.exp(running_max - new_max)
    running_sum = running_sum * fading + jnp.sum(attention_weights, axis=-1)
    output_accumulate = output_accumulate * fading[:, None] + jnp.dot(
        attention_weights.astype(jnp.bfloat16),
        slice_portion[:, :LATENT_WIDTH],
        preferred_element_type=jnp.float32,
    )
    final_state = (new_max, running_sum, output_accumulate)
    running_max, running_sum, output_accumulate = final_state
    out_latent = (
        (output_accumulate / running_sum[:, None])
        .astype(jnp.bfloat16)
        .reshape(count_of_rows, local_head_count, LATENT_WIDTH)
    )
    result = jnp.einsum(
        "rhc,hcv->rhv", out_latent, value_up_weight, preferred_element_type=jnp.float32
    ).astype(jnp.bfloat16)
    return result.reshape(1, count_of_rows, local_head_count * VALUE_HEAD_SIZE)


def solution(mesh):
    return jax.shard_map(
        local,
        mesh=mesh,
        in_specs=(
            P("role", "ctx", "head"),
            P("ctx", None),
            P(),
            P("ctx"),
            P("head", None),
            P("head", None),
            P(),
            P(),
            P(None, "head"),
            P("head", None, None),
            P("head", None, None),
        ),
        out_specs=P("role", "ctx", "head"),
        check_vma=False,
    )
```

profile of v0, /device:TPU:11, one launch (start us, length us, event | category | flops | bytes accessed | tf_op | source)
XLA Modules:
  0.0 112.0 jit_solution(4370328223607558288)
XLA Ops:
  6.5 0.0 copy-start
  6.5 0.0 reduce-scatter.3.cloned.1.call-start
  6.5 1.6 %copy-done = bf16[1792,576]{0,1:T(8,128)(2,1)S(1)} copy-done((bf16[1792,576]{0,1:T(8,128)(2,1)S(1)}, bf16[1792,576]{0,1:T(8,128)(2,1)}, u32[]{:S(2)}) %copy-start) | copy-done | bytes 2064408
  8.1 2.3 %fusion.23 = f32[64,576]{1,0:T(8,128)} fusion(bf16[1792,576]{0,1:T(8,128)(2,1)S(1)} %copy-done, bf16[1,64,1792]{2,1,0:T(8,128)(2,1)} %param.11), kind=kOutput, calls=%fused_computation.28 | convolution fusion | flops 132120576 | bytes 2441216 | tf_op jit(solution)/shard_map/dot_general | solution.py:74
  10.4 0.0 reduce-scatter.3.cloned.1.call-update
  10.5 0.0 copy-start.3
  10.5 0.0 copy-start.4
  10.5 0.0 reduce-scatter.5.cloned.1.call-start
  10.5 4.5 %fusion.21 = f32[64,1536]{1,0:T(8,128)} fusion(bf16[1792,1536]{1,0:T(8,128)(2,1)} %param.15, bf16[1,64,1792]{2,1,0:T(8,128)(2,1)} %param.11), kind=kOutput, calls=%fused_computation.26 | convolution fusion | flops 352321536 | bytes 6127616 | tf_op jit(solution)/shard_map/dot_general | solution.py:73
  15.1 0.0 reduce-scatter.5.cloned.1.call-update
  15.8 0.0 copy-done.6
  15.8 0.1 dynamic-slice_convert_fusion
  15.9 0.1 broadcast_in_dim.16
  15.9 0.1 lt.55
  16.1 0.2 multiply_cosine_fusion
  16.3 14.8 %reduce-scatter.3.cloned.1.call-done = f32[16,576]{1,0:T(8,128)} async-done(((f32[64,576]{1,0:T(8,128)}), f32[16,576]{1,0:T(8,128)}) %reduce-scatter.3.cloned.1.call-update) | async-done | bytes 36880 | tf_op jit(solution)/shard_map/reduce_scatter | solution.py:77
  31.0 0.9 multiply_reduce_fusion.2
  31.9 0.9 fusion.30
  32.8 0.0 copy-done.5
  32.8 0.8 multiply_convert_fusion.1
  33.6 0.1 pad_maximum_fusion.2
  33.7 6.2 %all_gather.9 = bf16[64,576]{1,0:T(8,128)(2,1)S(1)} all-gather(bf16[16,576]{1,0:T(8,128)(2,1)S(1)} %pad_maximum_fusion.2), channel_id=1, replica_groups=mesh['role'=2,'ctx'=4,'head'=4] {'head'}, dimensions={0}, use_global_device_ids=true | all-gather | bytes 92160 | tf_op jit(solution)/shard_map/all_gather | solution.py:88
  39.9 1.3 %collective-permute-start = (bf16[64,576]{1,0:T(8,128)(2,1)S(1)}, bf16[64,576]{1,0:T(8,128)(2,1)S(1)}, u32[]{:S(2)}, u32[]{:S(2)}) collective-permute-start(bf16[64,576]{1,0:T(8,128)(2,1)S(1)} %all_gather.9), channel_id=1, source_target_pairs={{0,16},{1,17},{2,18},{3,19},{4,20},{5,21},{6,22},{7,23},{8,24},{9,... | collective-permute-start | bytes 221192 | tf_op jit(solution)/shard_map/ppermute | solution.py:16
  41.3 4.4 %collective-permute-done = bf16[64,576]{1,0:T(8,128)(2,1)S(1)} collective-permute-done((bf16[64,576]{1,0:T(8,128)(2,1)S(1)}, bf16[64,576]{1,0:T(8,128)(2,1)S(1)}, u32[]{:S(2)}, u32[]{:S(2)}) %collective-permute-start) | collective-permute-done | bytes 73760 | tf_op jit(solution)/shard_map/ppermute | solution.py:16
  45.7 0.0 copy-done.3
  45.7 12.4 %all_gather.11 = bf16[448,576]{1,0:T(8,128)(2,1)S(1)} all-gather(bf16[112,576]{1,0:T(8,128)(2,1)S(1)} %pad_maximum_fusion.1), channel_id=1, replica_groups=mesh['role'=2,'ctx'=4,'head'=4] {'ctx'}, dimensions={0}, use_global_device_ids=true | all-gather | bytes 645120 | tf_op jit(solution)/shard_map/all_gather | solution.py:111
  58.1 1.0 multiply_reduce_fusion.1
  59.2 0.0 copy-done.4
  59.2 1.0 multiply_convert_fusion
  60.1 10.5 %all_gather.10 = bf16[64,1536]{1,0:T(8,128)(2,1)S(1)} all-gather(bf16[16,1536]{1,0:T(8,128)(2,1)S(1)} %multiply_convert_fusion), channel_id=1, replica_groups=mesh['role'=2,'ctx'=4,'head'=4] {'head'}, dimensions={0}, use_global_device_ids=true | all-gather | bytes 245760 | tf_op jit(solution)/shard_map/all_gather | solution.py:87
  70.6 11.0 %fusion.44 = f32[64,6144]{1,0:T(8,128)} fusion(bf16[64,1536]{1,0:T(8,128)(2,1)S(1)} %all_gather.10, bf16[1536,6144]{1,0:T(8,128)(2,1)} %param.19), kind=kOutput, calls=%fused_computation.75 | convolution fusion | flops 1207959552 | bytes 20643840 | tf_op jit(solution)/shard_map/dot_general | solution.py:90
  81.7 3.1 %reshape.145 = f32[64,32,192]{2,1,0:T(8,128)} reshape(f32[64,6144]{1,0:T(8,128)} %fusion.44) | data formatting | bytes 3145728 | tf_op jit(solution)/shard_map/reshape | solution.py:91
  84.8 2.1 %fusion.43 = (f32[64,32,32]{2,1,0:T(8,128)S(1)}, f32[64,32,32]{2,1,0:T(8,128)S(1)}) fusion(f32[64,32,192]{2,1,0:T(8,128)} %reshape.145), kind=kLoop, calls=%fused_computation.74 | loop fusion | bytes 1048576 | tf_op jit(solution)/shard_map/slice | solution.py:33
  86.9 1.3 %slice.43 = bf16[64,32,128]{2,1,0:T(8,128)(2,1)S(1)} slice(f32[64,32,192]{2,1,0:T(8,128)} %reshape.145), slice={[0:64], [0:32], [0:128]} | slice | bytes 1048576 | tf_op jit(solution)/shard_map/slice | solution.py:92
  88.2 0.7 convert_bitcast_fusion
  88.9 1.2 %subtract_convert_fusion = (bf16[64,32,32]{2,0,1:T(8,128)(2,1)S(1)}, bf16[64,32,32]{2,0,1:T(8,128)(2,1)S(1)}) fusion(f32[64,32,32]{2,1,0:T(8,128)S(1)} %get-tuple-element.14, f32[64,32,32]{2,1,0:T(8,128)S(1)} %get-tuple-element.13, f32[64,32]{1,0:T(8,128)S(1)} %get-tuple-element.20, f32[64,32]{1,0:T(8,128)S(1)} %get-tuple-element.19), kind=kLoop, calls=%fused_computation.24 | loop fusion | flops 524288 | bytes 802816 | tf_op jit(solution)/shard_map/convert
  90.2 0.9 multiply_reduce_fusion
  91.1 3.0 %copy.26 = bf16[64,32,576]{2,1,0:T(8,128)(2,1)} copy(bf16[64,32,576]{2,0,1:T(8,128)(2,1)S(1)} %get-tuple-element.8) | data formatting | bytes 4718592 | tf_op jit(solution)/shard_map/concatenate | solution.py:97
  94.1 0.1 copy.25
  94.2 0.1 mul.213
  94.3 3.6 %select_reduce_fusion = (f32[2048]{0:T(1024)S(1)}, f32[2048,448]{0,1:T(8,128)S(1)}) fusion(s32[2048]{0:T(1024)S(1)} %lt.55, s32[448]{0:T(512)S(1)} %add_select_fusion.2, pred[448]{0:T(512)(128)(4,1)S(1)} %compare_select_fusion, bf16[2048,576]{1,0:T(8,128)(2,1)} %bitcast.32, bf16[448,576]{1,0:T(8,128)(2,1)S(1)} %all_gather.11), kind=kOutput, calls=%fused_computation.6 | convolution fusion | flops 1061550080 | bytes 6564032 | tf_op jit(solution)/shard_map/dot_general | solution.py:128
  97.8 1.2 %fusion.3 = f32[2048]{0:T(1024)S(1)} fusion(f32[2048,448]{0,1:T(8,128)S(1)} %get-tuple-element.22, f32[2048]{0:T(1024)S(1)} %max.13, s32[2048]{0:T(1024)S(1)} %lt.55, s32[448]{0:T(512)S(1)} %add_select_fusion.2, pred[448]{0:T(512)(128)(4,1)S(1)} %compare_select_fusion), kind=kLoop, calls=%fused_computation.9 | loop fusion | flops 5502976 | bytes 3696832 | tf_op jit(solution)/shard_map/reduce_sum | solution.py:135
  99.1 0.0 copy-start.2
  99.1 2.0 %fusion.2 = bf16[2048,512]{1,0:T(8,128)(2,1)S(1)} fusion(f32[2048]{0:T(1024)S(1)} %get-tuple-element.5, f32[2048]{0:T(1024)S(1)} %get-tuple-element.6, f32[64,512]{1,0:T(8,128)S(1)} %slice_convert_fusion, f32[2048,448]{0,1:T(8,128)S(1)} %get-tuple-element.22, f32[2048]{0:T(1024)S(1)} %max.13, s32[2048]{0:T(1024)S(1)} %lt.55, s32[448]{0:T(512)S(1)} %add_select_fusion.2, ...), kind=kOutput, calls=%fused_computation.4 | convolution fusion | flops 949223424 | bytes 6392320 | tf_op jit(solution)/shard_map/dot_general | solution.py:136
  101.1 0.2 copy-done.2
  101.3 2.5 %fusion.17 = bf16[64,32,128]{2,0,1:T(8,128)(2,1)S(1)} fusion(bf16[32,512,128]{2,1,0:T(8,128)(2,1)S(1)} %copy-done.2, bf16[64,32,512]{2,1,0:T(8,128)(2,1)S(1)} %bitcast.31), kind=kOutput, calls=%fused_computation.21 | convolution fusion | flops 268697600 | bytes 6815744 | tf_op jit(solution)/shard_map/rhc,hcv->rhv/dot_general | solution.py:148
  103.8 0.3 copy.28
  104.2 1.0 reshape.148
  (17 shorter events, 0.1 us)
Async XLA Ops:
  6.5 1.6 %copy-start = (bf16[1792,576]{0,1:T(8,128)(2,1)S(1)}, bf16[1792,576]{0,1:T(8,128)(2,1)}, u32[]{:S(2)}) copy-start(bf16[1792,576]{0,1:T(8,128)(2,1)} %param.16) | copy-start | bytes 6193156
  6.5 24.5 %reduce-scatter.3.cloned.1.call-start = ((), (), s32[]{:S(2)}) async-start(), calls=%async_computation.2 | async-start | bytes 204800 | tf_op jit(solution)/shard_map/reduce_scatter | solution.py:77
  10.4 5.3 %copy-start.6 = (s32[64]{0:T(128)S(1)}, s32[64]{0:T(128)}, u32[]{:S(2)}) copy-start(s32[64]{0:T(128)} %param.14) | copy-start | bytes 772
  10.4 22.4 %copy-start.5 = (f32[512]{0:T(512)S(1)}, f32[512]{0:T(512)}, u32[]{:S(2)}) copy-start(f32[512]{0:T(512)} %param.18) | copy-start | bytes 6148
  10.5 35.2 %copy-start.3 = (bf16[48,576]{1,0:T(8,128)(2,1)S(1)}, bf16[48,576]{1,0:T(8,128)(2,1)}, u32[]{:S(2)}) copy-start(bf16[48,576]{1,0:T(8,128)(2,1)} %param.12) | copy-start | bytes 165892
  10.5 48.7 %copy-start.4 = (f32[1536]{0:T(1024)S(1)}, f32[1536]{0:T(1024)}, u32[]{:S(2)}) copy-start(f32[1536]{0:T(1024)} %param.17) | copy-start | bytes 18436
  10.5 47.6 %reduce-scatter.5.cloned.1.call-start = ((), (), s32[]{:S(2)}) async-start(), calls=%async_computation.3 | async-start | bytes 491520 | tf_op jit(solution)/shard_map/reduce_scatter | solution.py:76
  39.9 5.7 %collective-permute-start = (bf16[64,576]{1,0:T(8,128)(2,1)S(1)}, bf16[64,576]{1,0:T(8,128)(2,1)S(1)}, u32[]{:S(2)}, u32[]{:S(2)}) collective-permute-start(bf16[64,576]{1,0:T(8,128)(2,1)S(1)} %all_gather.9), channel_id=1, source_target_pairs={{0,16},{1,17},{2,18},{3,19},{4,20},{5,21},{6,22},{7,23},{8,24},{9,... | collective-permute-start | bytes 221192 | tf_op jit(solution)/shard_map/ppermute | solution.py:16
  84.8 3.4 %copy-start.1 = (bf16[32,128,512]{2,1,0:T(8,128)(2,1)S(1)}, bf16[32,128,512]{2,1,0:T(8,128)(2,1)}, u32[]{:S(2)}) copy-start(bf16[32,128,512]{2,1,0:T(8,128)(2,1)} %param.20) | copy-start | bytes 12582916
  99.1 2.2 %copy-start.2 = (bf16[32,512,128]{2,1,0:T(8,128)(2,1)S(1)}, bf16[32,512,128]{2,1,0:T(8,128)(2,1)}, u32[]{:S(2)}) copy-start(bf16[32,512,128]{2,1,0:T(8,128)(2,1)} %param.21) | copy-start | bytes 12582916
Sparse Core Ops, SparseCore 0:
  10.6 20.3 reduce-scatter.2
  33.5 21.1 reduce-scatter.4
where the time goes:
time: 113 us; the launch traced here: 112 us
  blocking collectives  29.1 us (26%)
  matrix products  26.7 us (24%)
  waiting for transfers between devices  19.2 us (17%)
  between operations  14.3 us (13%)
  local copies, waits for them, and re-layouts  13 us (12%)
  other arithmetic  8.49 us (8%)
  starting transfers between devices  1.32 us (1%)
    reduce_scatter x1, waiting for transfers between devices, local(): lax.psum_scatter(kv_part, 'head', scatter_dimension=0, tiled=True)  14.8 us
    all_gather x1, blocking collectives, local(): slice_portion = lax.all_gather(local_keys, 'ctx', axis=0, tiled=True)  12.4 us
    dot_general x1, matrix products, local(): queries = jnp.dot(query_norm, query_up, preferred_element_type=jnp.float32)  11 us
    all_gather x1, blocking collectives, local(): lax.all_gather(query_share, 'head', axis=0, tiled=True)  10.5 us
    all_gather x1, blocking collectives, local(): lax.all_gather(key_share, 'head', axis=0, tiled=True)  6.22 us
    dot_general x1, matrix products, local(): query_part = jnp.dot(inputs, query_down, preferred_element_type=jnp.float32)  4.52 us
    ppermute x1, waiting for transfers between devices, passed_along(): lax.ppermute(value, axis, [(source, source + steps) for source in range(l...  4.41 us
    dot_general x1, matrix products, local(): jnp.dot(flattened_query, slice_portion.T, preferred_element_type=jnp.floa...  3.55 us
  transfers between devices with their start and end apart: 3, of which 2 were waited for; matrix products, arithmetic and copies ran while one was open for 7% of the time, Pallas kernels for 0%

commit v1 on v0

--- a/solution.py
+++ b/solution.py
@@ -1,3 +1,4 @@
+import functools
 import jax
 import jax.numpy as jnp
 from jax import lax
@@ -8,6 +9,29 @@
 PLAIN_QUERY_DIM = 128
 VALUE_HEAD_SIZE = 128
 EPS = 1e-06
+
+
+def do_roots_by_axis(state, lane_axis):
+    panels = []
+    ndev = lax.axis_size(lane_axis)
+    for tick in [*range(ndev)]:
+        panels.append((tick, (tick + 1) % ndev))
+    entries = []
+    for tick in [*range(ndev)]:
+        entries.append((tick, (tick - 1) % ndev))
+    clean, oldest = ([state], [state])
+    for _ in range(ndev // 2):
+        opened = lax.ppermute(clean[-1], lane_axis, panels)
+        clean.append(opened)
+    for _ in tuple(range((ndev - 1) // 2)):
+        right_arr = lax.ppermute(oldest[-1], lane_axis, entries)
+        oldest.append(right_arr)
+    out_arr = jnp.concatenate([*clean[::-1], *oldest[1:]], 0)
+    built = lax.axis_index(lane_axis)
+    return jnp.roll(out_arr, (built - ndev // 2) * state.shape[0], 0)
+
+
+set_target = functools.partial(do_roots_by_axis, lane_axis="head")
 
 
 def passed_along(value, axis, steps):
@@ -85,7 +109,7 @@
     )
     query_norm, self_key_row = (
         lax.all_gather(query_share, "head", axis=0, tiled=True),
-        lax.all_gather(key_share, "head", axis=0, tiled=True),
+        set_target(key_share),
     )
     queries = jnp.dot(query_norm, query_up, preferred_element_type=jnp.float32)
     queries = queries.reshape(count_of_rows, local_head_count, PLAIN_QUERY_DIM + ROTARY_DIM)

time: 113 us -> 115 us (1.018)
  blocking collectives: 29.1 us -> 22.6 us
  waiting for transfers between devices: 19.2 us -> 23.7 us
  starting transfers between devices: 1.32 us -> 4.94 us
  matrix products: 26.7 us -> 24.9 us
  other arithmetic: 8.49 us -> 10.1 us
    all_gather x1 -> x0, blocking collectives: 6.22 us -> none  [local(): lax.all_gather(key_share, 'head', axis=0, tiled=True)]
    ppermute x0 -> x3, waiting for transfers between devices: none -> 3.99 us  [the longest x1 2.39 us: do_roots_by_axis(): right_arr = lax.ppermute(oldest[-1], lane_axis, entries)]
    ppermute x0 -> x3, starting transfers between devices: none -> 3.6 us  [the longest x2 3.6 us: do_roots_by_axis(): opened = lax.ppermute(clean[-1], lane_axis, panels)]
    dot_general x1, matrix products: 3.55 us -> 1.81 us  [local(): jnp.dot(flattened_query, slice_portion.T, preferred_element_type=jnp.floa...]
    reduce_sum x1, other arithmetic: 0.92 us -> 2.35 us  [local(): jnp.sum(complete_query.astype(jnp.float32) * self_key_row.astype(jnp.floa...]
  transfers between devices with their start and end apart: 3 -> 6, of which waited for: 2 -> 5; matrix products, arithmetic and copies ran while one was open for 7% -> 7% of each run, Pallas kernels for 0% -> 0%
where the time goes in v1:
time: 115 us; the launch traced here: 114 us
  matrix products  24.9 us (22%)
  waiting for transfers between devices  23.7 us (21%)
  blocking collectives  22.6 us (20%)
  between operations  14.3 us (12%)
  local copies, waits for them, and re-layouts  13.4 us (12%)
  other arithmetic  10.1 us (9%)
  starting transfers between devices  4.94 us (4%)
    reduce_scatter x1, waiting for transfers between devices, local(): lax.psum_scatter(kv_part, 'head', scatter_dimension=0, tiled=True)  14.9 us
    all_gather x1, blocking collectives, local(): slice_portion = lax.all_gather(local_keys, 'ctx', axis=0, tiled=True)  12.8 us
    dot_general x1, matrix products, local(): queries = jnp.dot(query_norm, query_up, preferred_element_type=jnp.float32)  11 us
    all_gather x1, blocking collectives, local(): lax.all_gather(query_share, 'head', axis=0, tiled=True)  9.84 us
    ppermute x1, waiting for transfers between devices, passed_along(): lax.ppermute(value, axis, [(source, source + steps) for source in range(l...  4.72 us
    dot_general x1, matrix products, local(): query_part = jnp.dot(inputs, query_down, preferred_element_type=jnp.float32)  4.52 us
    ppermute x2, starting transfers between devices, do_roots_by_axis(): opened = lax.ppermute(clean[-1], lane_axis, panels)  3.6 us
    concatenate x1, local copies, waits for them, and re-layouts, local(): complete_query = jnp.concatenate([absorbed, query_rot], axis=-1)  3.24 us
  transfers between devices with their start and end apart: 6, of which 5 were waited for; matrix products, arithmetic and copies ran while one was open for 7% of the time, Pallas kernels for 0%

profile of v1, /device:TPU:11, one launch (start us, length us, event | category | flops | bytes accessed | tf_op | source)
XLA Modules:
  0.0 113.9 jit_solution(10646808280714123797)
XLA Ops:
  6.5 1.6 %copy-done = bf16[1792,576]{0,1:T(8,128)(2,1)S(1)} copy-done((bf16[1792,576]{0,1:T(8,128)(2,1)S(1)}, bf16[1792,576]{0,1:T(8,128)(2,1)}, u32[]{:S(2)}) %copy-start) | copy-done | bytes 2064408
  8.1 2.3 %fusion.24 = f32[64,576]{1,0:T(8,128)} fusion(bf16[1792,576]{0,1:T(8,128)(2,1)S(1)} %copy-done, bf16[1,64,1792]{2,1,0:T(8,128)(2,1)} %param.11), kind=kOutput, calls=%fused_computation.29 | convolution fusion | flops 132120576 | bytes 2441216 | tf_op jit(solution)/shard_map/dot_general | solution.py:98
  10.5 0.0 reduce-scatter.3.cloned.1.call-update
  10.5 0.0 copy-start.4
  10.5 0.0 reduce-scatter.5.cloned.1.call-start
  10.6 4.5 %fusion.22 = f32[64,1536]{1,0:T(8,128)} fusion(bf16[1792,1536]{1,0:T(8,128)(2,1)} %param.15, bf16[1,64,1792]{2,1,0:T(8,128)(2,1)} %param.11), kind=kOutput, calls=%fused_computation.27 | convolution fusion | flops 352321536 | bytes 6127616 | tf_op jit(solution)/shard_map/dot_general | solution.py:97
  15.1 0.0 reduce-scatter.5.cloned.1.call-update
  15.8 0.1 dynamic-slice_convert_fusion.1
  15.9 0.2 multiply_cosine_fusion
  16.1 14.9 %reduce-scatter.3.cloned.1.call-done = f32[16,576]{1,0:T(8,128)} async-done(((f32[64,576]{1,0:T(8,128)}), f32[16,576]{1,0:T(8,128)}) %reduce-scatter.3.cloned.1.call-update) | async-done | bytes 36880 | tf_op jit(solution)/shard_map/reduce_scatter | solution.py:101
  31.0 0.9 multiply_reduce_fusion.2
  31.9 0.9 fusion.31
  32.8 0.8 multiply_convert_fusion.1
  33.6 0.1 pad_maximum_fusion.2
  33.7 1.3 %collective-permute-start = (bf16[16,576]{1,0:T(8,128)(2,1)S(1)}, bf16[16,576]{1,0:T(8,128)(2,1)S(1)}, u32[]{:S(2)}, u32[]{:S(2)}) collective-permute-start(bf16[16,576]{1,0:T(8,128)(2,1)S(1)} %pad_maximum_fusion.2), channel_id=1, source_target_pairs={{0,1},{1,2},{2,3},{3,0},{4,5},{5,6},{6,7},{7,4},{8,9},{9,10},{10,1... | collective-permute-start | bytes 55304 | tf_op jit(solution)/shard_map/ppermute | solution.py:24
  35.0 0.9 collective-permute-done
  35.9 2.3 %collective-permute-start.1 = (bf16[16,576]{1,0:T(8,128)(2,1)S(1)}, bf16[16,576]{1,0:T(8,128)(2,1)S(1)}, u32[]{:S(2)}, u32[]{:S(2)}) collective-permute-start(bf16[16,576]{1,0:T(8,128)(2,1)S(1)} %collective-permute-done), channel_id=1, source_target_pairs={{0,1},{1,2},{2,3},{3,0},{4,5},{5,6},{6,7},{7,4},{8,9},{9,10},{10,1... | collective-permute-start | bytes 55304 | tf_op jit(solution)/shard_map/ppermute | solution.py:24
  38.3 0.1 broadcast_in_dim.16
  38.3 0.1 lt.69
  38.4 0.0 collective-permute-start.2
  38.4 0.7 collective-permute-done.1
  39.2 0.1 constant_dynamic-update-slice_fusion.5
  39.2 2.4 %collective-permute-done.2 = bf16[16,576]{1,0:T(8,128)(2,1)S(1)} collective-permute-done((bf16[16,576]{1,0:T(8,128)(2,1)S(1)}, bf16[16,576]{1,0:T(8,128)(2,1)S(1)}, u32[]{:S(2)}, u32[]{:S(2)}) %collective-permute-start.2) | collective-permute-done | bytes 18464 | tf_op jit(solution)/shard_map/ppermute | solution.py:27
  41.7 0.1 constant_dynamic-update-slice_fusion.1
  41.8 1.3 %collective-permute-start.3 = (bf16[64,576]{1,0:T(8,128)(2,1)S(1)}, bf16[64,576]{1,0:T(8,128)(2,1)S(1)}, u32[]{:S(2)}, u32[]{:S(2)}) collective-permute-start(bf16[64,576]{1,0:T(8,128)(2,1)S(1)} %get-tuple-element.10), channel_id=1, source_target_pairs={{0,16},{1,17},{2,18},{3,19},{4,20},{5,21},{6,22},{7,23},{8,24},{9,... | collective-permute-start | bytes 221192 | tf_op jit(solution)/shard_map/ppermute | solution.py:40
  43.1 4.7 %collective-permute-done.3 = bf16[64,576]{1,0:T(8,128)(2,1)S(1)} collective-permute-done((bf16[64,576]{1,0:T(8,128)(2,1)S(1)}, bf16[64,576]{1,0:T(8,128)(2,1)S(1)}, u32[]{:S(2)}, u32[]{:S(2)}) %collective-permute-start.3) | collective-permute-done | bytes 73760 | tf_op jit(solution)/shard_map/ppermute | solution.py:40
  47.9 12.8 %all_gather.7 = bf16[448,576]{1,0:T(8,128)(2,1)S(1)} all-gather(bf16[112,576]{1,0:T(8,128)(2,1)S(1)} %pad_maximum_fusion.1), channel_id=1, replica_groups=mesh['role'=2,'ctx'=4,'head'=4] {'ctx'}, dimensions={0}, use_global_device_ids=true | all-gather | bytes 645120 | tf_op jit(solution)/shard_map/all_gather | solution.py:135
  60.6 1.0 multiply_reduce_fusion.1
  61.7 1.0 multiply_convert_fusion
  62.7 9.8 %all_gather.6 = bf16[64,1536]{1,0:T(8,128)(2,1)S(1)} all-gather(bf16[16,1536]{1,0:T(8,128)(2,1)S(1)} %multiply_convert_fusion), channel_id=1, replica_groups=mesh['role'=2,'ctx'=4,'head'=4] {'head'}, dimensions={0}, use_global_device_ids=true | all-gather | bytes 245760 | tf_op jit(solution)/shard_map/all_gather | solution.py:111
  72.5 11.0 %fusion.46 = f32[64,6144]{1,0:T(8,128)} fusion(bf16[64,1536]{1,0:T(8,128)(2,1)S(1)} %all_gather.6, bf16[1536,6144]{1,0:T(8,128)(2,1)} %param.19), kind=kOutput, calls=%fused_computation.86 | convolution fusion | flops 1207959552 | bytes 20643840 | tf_op jit(solution)/shard_map/dot_general | solution.py:114
  83.5 3.1 %reshape.145 = f32[64,32,192]{2,1,0:T(8,128)} reshape(f32[64,6144]{1,0:T(8,128)} %fusion.46) | data formatting | bytes 3145728 | tf_op jit(solution)/shard_map/reshape | solution.py:115
  86.7 1.5 %slice.42 = bf16[64,32,128]{2,1,0:T(8,128)(2,1)S(1)} slice(f32[64,32,192]{2,1,0:T(8,128)} %reshape.145), slice={[0:64], [0:32], [0:128]} | slice | bytes 1048576 | tf_op jit(solution)/shard_map/slice | solution.py:116
  88.2 2.0 %fusion.45 = (f32[64,32,32]{2,1,0:T(8,128)S(1)}, f32[64,32,32]{2,1,0:T(8,128)S(1)}) fusion(f32[64,32,192]{2,1,0:T(8,128)} %reshape.145), kind=kLoop, calls=%fused_computation.85 | loop fusion | bytes 1048576 | tf_op jit(solution)/shard_map/slice | solution.py:57
  90.2 0.7 convert_bitcast_fusion
  90.9 1.2 %subtract_convert_fusion = (bf16[64,32,32]{2,0,1:T(8,128)(2,1)S(1)}, bf16[64,32,32]{2,0,1:T(8,128)(2,1)S(1)}) fusion(f32[64,32,32]{2,1,0:T(8,128)S(1)} %get-tuple-element.16, f32[64,32,32]{2,1,0:T(8,128)S(1)} %get-tuple-element.15, f32[64,32]{1,0:T(8,128)S(1)} %get-tuple-element.20, f32[64,32]{1,0:T(8,128)S(1)} %get-tuple-element.19), kind=kLoop, calls=%fused_computation.25 | loop fusion | flops 524288 | bytes 802816 | tf_op jit(solution)/shard_map/convert
  92.2 2.4 %multiply_reduce_fusion = (f32[64,32]{0,1:T(8,128)S(1)}, bf16[64,32,576]{2,0,1:T(8,128)(2,1)}) fusion(f32[64,576]{1,0:T(8,128)S(1)} %get-tuple-element.9, bf16[64,32,32]{2,0,1:T(8,128)(2,1)S(1)} %get-tuple-element.14, bf16[64,32,32]{2,0,1:T(8,128)(2,1)S(1)} %get-tuple-element.13, bf16[64,32,512]{2,0,1:T(8,128)(2,1)S(1)} %convert_bitcast_fusion), kind=kLoop, calls=%fused_computation | loop fusion | flops 10614784 | bytes 4874240 | tf_op jit(solution)/shard_map/reduce_sum | solution.py:123
  94.5 0.1 copy.25
  94.6 0.1 mul.217
  94.7 3.2 %copy.26 = bf16[64,32,576]{2,1,0:T(8,128)(2,1)S(1)} copy(bf16[64,32,576]{2,0,1:T(8,128)(2,1)} %get-tuple-element.8) | data formatting | bytes 4718592 | tf_op jit(solution)/shard_map/concatenate | solution.py:121
  97.9 1.8 %select_reduce_fusion = (f32[2048]{0:T(1024)S(1)}, f32[2048,448]{0,1:T(8,128)S(1)}) fusion(s32[2048]{0:T(1024)S(1)} %lt.69, s32[448]{0:T(512)S(1)} %add_select_fusion.2, pred[448]{0:T(512)(128)(4,1)S(1)} %compare_select_fusion, bf16[2048,576]{1,0:T(8,128)(2,1)S(1)} %bitcast.32, bf16[448,576]{1,0:T(8,128)(2,1)S(1)} %all_gather.7), kind=kOutput, calls=%fused_computation.6 | convolution fusion | flops 1061550080 | bytes 6564032 | tf_op jit(solution)/shard_map/dot_general | solution.py:152
  99.8 1.2 %fusion.3 = f32[2048]{0:T(1024)S(1)} fusion(f32[2048,448]{0,1:T(8,128)S(1)} %get-tuple-element.22, f32[2048]{0:T(1024)S(1)} %max.13, s32[2048]{0:T(1024)S(1)} %lt.69, s32[448]{0:T(512)S(1)} %add_select_fusion.2, pred[448]{0:T(512)(128)(4,1)S(1)} %compare_select_fusion), kind=kLoop, calls=%fused_computation.9 | loop fusion | flops 5502976 | bytes 3696832 | tf_op jit(solution)/shard_map/reduce_sum | solution.py:159
  101.0 0.0 copy-start.2
  101.0 2.0 %fusion.2 = bf16[2048,512]{1,0:T(8,128)(2,1)S(1)} fusion(f32[2048]{0:T(1024)S(1)} %get-tuple-element.5, f32[2048]{0:T(1024)S(1)} %get-tuple-element.6, f32[64,512]{1,0:T(8,128)S(1)} %dynamic-slice_convert_fusion, bf16[448,576]{1,0:T(8,128)(2,1)S(1)} %all_gather.7, f32[2048,448]{0,1:T(8,128)S(1)} %get-tuple-element.22, f32[2048]{0:T(1024)S(1)} %max.13, ...), kind=kOutput, calls=%fused_computation.4 | convolution fusion | flops 949223424 | bytes 6392320 | tf_op jit(solution)/shard_map/dot_general | solution.py:160
  103.0 0.2 copy-done.2
  103.2 2.5 %fusion.18 = bf16[64,32,128]{2,0,1:T(8,128)(2,1)S(1)} fusion(bf16[32,512,128]{2,1,0:T(8,128)(2,1)S(1)} %copy-done.2, bf16[64,32,512]{2,1,0:T(8,128)(2,1)S(1)} %bitcast.31), kind=kOutput, calls=%fused_computation.22 | convolution fusion | flops 268697600 | bytes 6815744 | tf_op jit(solution)/shard_map/rhc,hcv->rhv/dot_general | solution.py:172
  105.7 0.3 copy.28
  106.1 1.0 reshape.148
  (31 shorter events, 0.2 us)
Async XLA Ops:
  6.5 1.6 %copy-start = (bf16[1792,576]{0,1:T(8,128)(2,1)S(1)}, bf16[1792,576]{0,1:T(8,128)(2,1)}, u32[]{:S(2)}) copy-start(bf16[1792,576]{0,1:T(8,128)(2,1)} %param.16) | copy-start | bytes 6193156
  6.5 24.5 %reduce-scatter.3.cloned.1.call-start = ((), (), s32[]{:S(2)}) async-start(), calls=%async_computation.2 | async-start | bytes 204800 | tf_op jit(solution)/shard_map/reduce_scatter | solution.py:101
  10.4 5.3 %copy-start.6 = (s32[64]{0:T(128)S(1)}, s32[64]{0:T(128)}, u32[]{:S(2)}) copy-start(s32[64]{0:T(128)} %param.14) | copy-start | bytes 772
  10.5 22.4 %copy-start.5 = (f32[512]{0:T(512)S(1)}, f32[512]{0:T(512)}, u32[]{:S(2)}) copy-start(f32[512]{0:T(512)} %param.18) | copy-start | bytes 6148
  10.5 37.4 %copy-start.3 = (bf16[48,576]{1,0:T(8,128)(2,1)S(1)}, bf16[48,576]{1,0:T(8,128)(2,1)}, u32[]{:S(2)}) copy-start(bf16[48,576]{1,0:T(8,128)(2,1)} %param.12) | copy-start | bytes 165892
  10.5 51.2 %copy-start.4 = (f32[1536]{0:T(1024)S(1)}, f32[1536]{0:T(1024)}, u32[]{:S(2)}) copy-start(f32[1536]{0:T(1024)} %param.17) | copy-start | bytes 18436
  10.5 50.1 %reduce-scatter.5.cloned.1.call-start = ((), (), s32[]{:S(2)}) async-start(), calls=%async_computation.3 | async-start | bytes 491520 | tf_op jit(solution)/shard_map/reduce_scatter | solution.py:100
  33.7 2.2 %collective-permute-start = (bf16[16,576]{1,0:T(8,128)(2,1)S(1)}, bf16[16,576]{1,0:T(8,128)(2,1)S(1)}, u32[]{:S(2)}, u32[]{:S(2)}) collective-permute-start(bf16[16,576]{1,0:T(8,128)(2,1)S(1)} %pad_maximum_fusion.2), channel_id=1, source_target_pairs={{0,1},{1,2},{2,3},{3,0},{4,5},{5,6},{6,7},{7,4},{8,9},{9,10},{10,1... | collective-permute-start | bytes 55304 | tf_op jit(solution)/shard_map/ppermute | solution.py:24
  35.9 3.2 %collective-permute-start.1 = (bf16[16,576]{1,0:T(8,128)(2,1)S(1)}, bf16[16,576]{1,0:T(8,128)(2,1)S(1)}, u32[]{:S(2)}, u32[]{:S(2)}) collective-permute-start(bf16[16,576]{1,0:T(8,128)(2,1)S(1)} %collective-permute-done), channel_id=1, source_target_pairs={{0,1},{1,2},{2,3},{3,0},{4,5},{5,6},{6,7},{7,4},{8,9},{9,10},{10,1... | collective-permute-start | bytes 55304 | tf_op jit(solution)/shard_map/ppermute | solution.py:24
  38.4 3.2 %collective-permute-start.2 = (bf16[16,576]{1,0:T(8,128)(2,1)S(1)}, bf16[16,576]{1,0:T(8,128)(2,1)S(1)}, u32[]{:S(2)}, u32[]{:S(2)}) collective-permute-start(bf16[16,576]{1,0:T(8,128)(2,1)S(1)} %pad_maximum_fusion.2), channel_id=1, source_target_pairs={{0,3},{1,0},{2,1},{3,2},{4,7},{5,4},{6,5},{7,6},{8,11},{9,8},{10,9... | collective-permute-start | bytes 55304 | tf_op jit(solution)/shard_map/ppermute | solution.py:27
  41.8 6.0 %collective-permute-start.3 = (bf16[64,576]{1,0:T(8,128)(2,1)S(1)}, bf16[64,576]{1,0:T(8,128)(2,1)S(1)}, u32[]{:S(2)}, u32[]{:S(2)}) collective-permute-start(bf16[64,576]{1,0:T(8,128)(2,1)S(1)} %get-tuple-element.10), channel_id=1, source_target_pairs={{0,16},{1,17},{2,18},{3,19},{4,20},{5,21},{6,22},{7,23},{8,24},{9,... | collective-permute-start | bytes 221192 | tf_op jit(solution)/shard_map/ppermute | solution.py:40
  86.7 3.5 %copy-start.1 = (bf16[32,128,512]{2,1,0:T(8,128)(2,1)S(1)}, bf16[32,128,512]{2,1,0:T(8,128)(2,1)}, u32[]{:S(2)}) copy-start(bf16[32,128,512]{2,1,0:T(8,128)(2,1)} %param.20) | copy-start | bytes 12582916
  101.0 2.2 %copy-start.2 = (bf16[32,512,128]{2,1,0:T(8,128)(2,1)S(1)}, bf16[32,512,128]{2,1,0:T(8,128)(2,1)}, u32[]{:S(2)}) copy-start(bf16[32,512,128]{2,1,0:T(8,128)(2,1)} %param.21) | copy-start | bytes 12582916
Sparse Core Ops, SparseCore 0:
  10.6 20.3 reduce-scatter.2
  33.5 21.1 reduce-scatter.4
